TPU v7x, 32 devices: a whole 2x2x4 slice. The times are simulated.
32 devices in a mesh: groups: 2 (over y), gx: 4 (over z), gy: 4 (over x, core).
Axes of the slice: x: 2, y: 2, z: 4, core: 2. Of those that a mesh axis runs over, the one named last changes fastest.
Arguments:
- tokens: bfloat16 [2, 16, 16384], P(None, 'groups', 'gx'), parts along dimension 1, may hold values from -20 to 20, as said below
- lengths: int32 [2, 16], P(None, ('groups', 'gx')), parts along dimension 1, may hold values from 1 to 1024, as said below
- norm_gain: bfloat16 [16384], P('gx'), may hold values from 0.5 to 2
- w_query: bfloat16 [16384, 8192], P('gx', 'gy'), may hold values from -1.171875 to 1.171875
- key_value_weight: bfloat16 [16384, 4, 256], P('gx', 'gy'), may hold values from -0.046875 to 0.046875
- w_out: bfloat16 [8192, 16384], P('gy', 'gx'), may hold values from -0.0625 to 0.0625
- cache: bfloat16 [2, 16, 1024, 4, 2, 128], P(None, ('groups', 'gx'), None, 'gy'), parts along dimension 1, may hold values from -16 to 16
Outputs:
- layer_out: bfloat16 [2, 16, 16384], P(None, 'groups', 'gx'), parts along dimension 1
There are 2 independent parts, one for each index of `groups`. A program takes and returns all parts, laid end to end along the dimension named above; an argument that names none is the same for every part. Nothing has to cross between parts.
Inputs may be any that keep to these rules, and one draw needn't show every extreme that they name: `tokens`: entries vary with the feature and the row. `lengths`: some rollout has exactly 1024 cached positions in every draw.
All inputs are finite; a program needn't handle non-finite values.
Results may differ from a plain program's by a relative error of at most 0.012.
The roundings to bfloat16 on the way count: a program that leaves them out, or rounds other values in their place, can miss the bound.
Values may be sent and summed in bfloat16 or wider, within the bound.
No kernel may reach another device: no remote copies, remote signals or barrier semaphores. Data moves between devices by JAX's collectives and lax.ppermute only.
A program may use at most 128 MiB of HBM per device.

v0:
```python
import jax
import jax.numpy as jnp
from jax import lax
from jax.sharding import PartitionSpec as P

MODEL_WIDTH = 16384
HEAD_SIZE = 128


def rotate(vectors, positions):
    half = vectors.shape[-1] // 2
    freq = 500000.0 ** (-2.0 * jnp.arange(half, dtype=jnp.float32) / vectors.shape[-1])
    angle = positions[..., None] * freq
    cosine = jnp.cos(angle)
    sine = jnp.sin(angle)
    first = vectors[..., :half]
    second = vectors[..., half:]
    return jnp.concatenate(
        [first * cosine - second * sine, second * cosine + first * sine], axis=-1
    )


def attend(query_sum, keyval_sum, local_squares, lengths, cache):
    batches, rows_here = lengths.shape
    score_scale = lax.rsqrt(local_squares / MODEL_WIDTH + 1e-05)
    heads_kv = keyval_sum.shape[2]
    query_group = query_sum.shape[2] // (heads_kv * HEAD_SIZE)
    query = (
        query_sum.reshape(batches, rows_here, heads_kv, query_group, HEAD_SIZE)
        * score_scale[:, :, None, None, None]
    )
    key_value = keyval_sum * score_scale[:, :, None, None]
    positions = lengths.astype(jnp.float32)
    rotated_query = rotate(query, positions[:, :, None, None]).astype(jnp.bfloat16)
    rkey = rotate(key_value[..., :HEAD_SIZE], positions[:, :, None])
    value_new = key_value[..., HEAD_SIZE:]
    inv_root = 1.0 / jnp.sqrt(jnp.float32(HEAD_SIZE))
    keys = cache[:, :, :, :, 0, :]
    values = cache[:, :, :, :, 1, :]
    scores = (
        jnp.einsum("mrkgd,mrskd->mrkgs", rotated_query, keys, preferred_element_type=jnp.float32)
        * inv_root
    )
    valid = jnp.arange(cache.shape[2], dtype=jnp.int32)[None, None, :] < lengths[:, :, None]
    scores = jnp.where(valid[:, :, None, None, :], scores, -1e30)
    new_score = (
        jnp.sum(rotated_query.astype(jnp.float32) * rkey[:, :, :, None, :], axis=-1) * inv_root
    )
    top = jnp.maximum(jnp.max(scores, axis=-1), new_score)
    weights = jnp.exp(scores - top[..., None])
    new_weight = jnp.exp(new_score - top)
    total = jnp.sum(weights, axis=-1) + new_weight
    summed = jnp.einsum(
        "mrkgs,mrskd->mrkgd",
        weights.astype(jnp.bfloat16),
        values,
        preferred_element_type=jnp.float32,
    )
    summed = summed + new_weight[..., None] * value_new[:, :, :, None, :]
    return (
        (summed / total[..., None])
        .astype(jnp.bfloat16)
        .reshape(batches, rows_here, heads_kv * query_group * HEAD_SIZE)
    )


def local(tokens, lengths, norm_gain, w_query, key_value_weight, w_out, cache):
    x_full = tokens.astype(jnp.float32)
    squares = jnp.sum(x_full * x_full, axis=-1)
    normed = (x_full * norm_gain.astype(jnp.float32)).astype(jnp.bfloat16)
    query_part = jnp.einsum("mrd,dc->mrc", normed, w_query, preferred_element_type=jnp.float32)
    keyval_part = jnp.einsum(
        "mrd,dkc->mrkc", normed, key_value_weight, preferred_element_type=jnp.float32
    )
    query_sum, keyval_sum, local_squares = (
        lax.psum_scatter(query_part, "gx", scatter_dimension=1, tiled=True),
        lax.psum_scatter(keyval_part, "gx", scatter_dimension=1, tiled=True),
        lax.psum_scatter(squares, "gx", scatter_dimension=1, tiled=True),
    )
    attended = attend(query_sum, keyval_sum, local_squares, lengths, cache)
    projected = jnp.einsum(
        "mrc,cd->mrd",
        lax.all_gather(attended, "gx", axis=1, tiled=True),
        w_out,
        preferred_element_type=jnp.float32,
    )
    summed_heads = lax.psum(projected, "gy")
    return (x_full + summed_heads).astype(jnp.bfloat16)


def solution(mesh):
    placed = (
        P(None, "groups", "gx"),
        P(None, ("groups", "gx")),
        P("gx"),
        P("gx", "gy"),
        P("gx", "gy", None),
        P("gy", "gx"),
        P(None, ("groups", "gx"), None, "gy", None, None),
    )
    return jax.shard_map(
        local, mesh=mesh, in_specs=placed, out_specs=P(None, "groups", "gx"), check_vma=False
    )
```

profile of v0, /device:TPU:0, one launch (start us, length us, event | category | flops | bytes accessed | tf_op | source)
XLA Modules:
  0.0 122.0 jit_solution(11372717634072038642)
XLA Ops:
  6.5 0.0 copy-start
  6.5 0.0 all-reduce.9.cloned.1.call-start
  6.5 0.8 convert_element_type.46
  7.4 0.0 copy-start.1
  7.4 0.0 copy-start.2
  7.4 8.8 %fusion.2 = f32[2,8,2048]{2,1,0:T(8,128)} fusion(bf16[4096,2048]{1,0:T(8,128)(2,1)} %param.10, bf16[2,8,4096]{2,1,0:T(8,128)(2,1)} %param.7, f32[4096]{0:T(1024)S(1)} %convert_element_type.46), kind=kOutput, calls=%fused_computation.2 | convolution fusion | flops 268632064 | bytes 17055744 | tf_op jit(solution)/shard_map/mrd,dc->mrc/dot_general | solution.py:71
  16.2 0.0 copy-start.3
  16.2 0.0 all-reduce.9.cloned.1.call-update
  16.2 0.0 all-reduce.7.cloned.1.call-start
  16.3 0.0 copy-done.1
  16.3 0.1 fusion.13
  16.4 0.0 copy-done.2
  16.4 0.1 iota_compare_fusion
  16.5 0.0 copy-done
  16.5 0.4 fusion.9
  16.9 0.0 copy-done.3
  16.9 0.7 dynamic-slice
  18.3 0.1 multiply_cosine_fusion.1
  18.4 20.8 %all-reduce.3 = (f32[2,8]{1,0:T(2,128)S(1)}, f32[2,8,1,256]{3,1,0,2:T(8,128)S(1)}) all-reduce(f32[2,8]{1,0:T(2,128)S(1)} %fusion.13, f32[2,8,1,256]{3,1,0,2:T(8,128)S(1)} %fusion.9), channel_id=3, replica_groups=mesh['groups'=2,'gx'=4,'gy'=4] {'gx'}, use_global_device_ids=true, to_apply=%region_2.0.clone | all-reduce | flops 4112 | bytes 32896
  39.2 0.1 fusion.32
  39.3 0.1 dynamic-slice_multiply_fusion
  39.4 0.1 fusion.29
  39.5 6.9 %fusion.35 = (bf16[2,2,1024,1,1,128]{5,4,3,2,1,0:T(2,128)(2,1)}, bf16[2,2,1024,1,1,128]{5,4,3,2,1,0:T(2,128)(2,1)}) fusion(bf16[2,2,1024,1,2,128]{5,4,3,2,1,0:T(2,128)(2,1)} %param.13), kind=kLoop, calls=%fused_computation.55 | loop fusion | bytes 4194304 | tf_op jit(solution)/shard_map/slice | solution.py:38
  46.4 0.1 maximum_bitcast_fusion
  46.5 7.3 %all-reduce.9.cloned.1.call-done = f32[2,8,2048]{2,1,0:T(8,128)} async-done(((f32[2,8,2048]{2,1,0:T(8,128)}), f32[2,8,2048]{2,1,0:T(8,128)}) %all-reduce.9.cloned.1.call-update) | async-done | bytes 131088
  53.9 0.9 constant_dynamic-slice_fusion
  54.8 0.1 broadcast_multiply_fusion
  54.9 0.1 subtract_convert_fusion
  55.0 0.2 multiply_reduce_fusion
  55.1 2.1 %fusion.36 = (f32[2,2,16]{2,1,0:T(2,128)S(1)}, f32[2,2,16,1024]{3,2,1,0:T(8,128)S(1)}) fusion(bf16[2,2,1024,1,1,128]{5,4,3,2,1,0:T(2,128)(2,1)} %get-tuple-element.9, bf16[2,2,16,64]{3,2,1,0:T(8,128)(2,1)S(1)} %bitcast.38, bf16[2,2,16,64]{3,2,1,0:T(8,128)(2,1)S(1)} %bitcast.37, pred[2,2,1024]{2,1,0:T(4,128)(4,1)S(1)} %iota_compare_fusion), kind=kOutput, calls=%fused_computation.56 | convolution fusion | flops 17006528 | bytes 1331456 | tf_op jit(solution)/shard_map/mrkgd,mrskd->mrkgs/dot_general | solution.py:41
  57.3 0.2 fusion.15
  57.5 1.9 %fusion.8 = bf16[2,2,16,128]{3,2,1,0:T(8,128)(2,1)S(1)} fusion(bf16[2,2,1024,1,1,128]{5,4,3,2,1,0:T(2,128)(2,1)} %get-tuple-element.10, f32[2,2,16,1024]{3,2,1,0:T(8,128)S(1)} %get-tuple-element.18, f32[2,2,16]{2,1,0:T(2,128)S(1)} %multiply_maximum_fusion, f32[2,2,16]{2,1,0:T(2,128)S(1)} %get-tuple-element.7, f32[2,2,128]{2,1,0:T(2,128)S(1)} %slice_bitcast_fusion, ...), kind=kOutput, calls=%fused_computation.10 | convolution fusion | flops 16941056 | bytes 1329920 | tf_op jit(solution)/shard_map/mrkgs,mrskd->mrkgd/dot_general | solution.py:53
  59.4 13.1 %all_gather.3 = bf16[2,8,2048]{2,0,1:T(2,128)(2,1)S(1)} all-gather(bf16[2,2,2048]{2,0,1:T(2,128)(2,1)S(1)} %copy.12), channel_id=1, replica_groups=mesh['groups'=2,'gx'=4,'gy'=4] {'gx'}, dimensions={1}, use_global_device_ids=true | all-gather | bytes 81920 | tf_op jit(solution)/shard_map/all_gather | solution.py:83
  72.6 8.8 %fusion = f32[2,8,4096]{2,1,0:T(8,128)} fusion(bf16[2048,4096]{1,0:T(8,128)(2,1)} %param.12, bf16[2,8,2048]{2,0,1:T(2,128)(2,1)S(1)} %all_gather.3), kind=kOutput, calls=%fused_computation | convolution fusion | flops 268435456 | bytes 17104896 | tf_op jit(solution)/shard_map/mrc,cd->mrd/dot_general | solution.py:81
  81.3 0.0 all-reduce.7.cloned.1.call-update
  81.3 32.2 %all-reduce.7.cloned.1.call-done = f32[2,8,4096]{2,1,0:T(8,128)} async-done(((f32[2,8,4096]{2,1,0:T(8,128)}), f32[2,8,4096]{2,1,0:T(8,128)}) %all-reduce.7.cloned.1.call-update) | async-done | bytes 262160 | tf_op jit(solution)/shard_map/psum | solution.py:87
  113.5 1.6 %fusion.14 = bf16[2,8,4096]{2,1,0:T(8,128)(2,1)} fusion(f32[2,8,4096]{2,1,0:T(8,128)} %all-reduce.7.cloned.1.call-done, bf16[2,8,4096]{2,1,0:T(8,128)(2,1)S(1)} %copy-done.1), kind=kLoop, calls=%fused_computation.19 | loop fusion | flops 196608 | bytes 524288 | tf_op jit(solution)/shard_map/convert_element_type | solution.py:88
  (8 shorter events, 0.1 us)
Async XLA Ops:
  6.5 10.0 %copy-start = (bf16[4096,1,256]{2,0,1:T(8,128)(2,1)S(1)}, bf16[4096,1,256]{2,0,1:T(8,128)(2,1)}, u32[]{:S(2)}) copy-start(bf16[4096,1,256]{2,0,1:T(8,128)(2,1)} %param.11) | copy-start | bytes 6291460
  6.5 47.3 %all-reduce.9.cloned.1.call-start = ((), (), s32[]{:S(2)}) async-start(), calls=%async_computation.1 | async-start | bytes 262144
  7.4 8.9 %copy-start.1 = (bf16[2,8,4096]{2,1,0:T(8,128)(2,1)S(1)}, bf16[2,8,4096]{2,1,0:T(8,128)(2,1)}, u32[]{:S(2)}) copy-start(bf16[2,8,4096]{2,1,0:T(8,128)(2,1)} %param.7) | copy-start | bytes 393220
  7.4 9.0 %copy-start.2 = (s32[2,2]{1,0:T(2,128)S(1)}, s32[2,2]{1,0:T(2,128)}, u32[]{:S(2)}) copy-start(s32[2,2]{1,0:T(2,128)} %param.8) | copy-start | bytes 52
  16.2 0.7 copy-start.3
  16.2 97.3 %all-reduce.7.cloned.1.call-start = ((), (), s32[]{:S(2)}) async-start(), calls=%async_computation | async-start | bytes 524288 | tf_op jit(solution)/shard_map/psum | solution.py:87
Sparse Core Ops, SparseCore 0:
  16.4 37.4 all-reduce.8
  81.5 31.9 all-reduce.6
where the time goes:
time: 122 us
  waiting for transfers between devices  39.5 us (32%)
  blocking collectives  33.9 us (28%)
  matrix products  22 us (18%)
  between operations  14.2 us (12%)
  local copies, waits for them, and re-layouts  8.61 us (7%)
  other arithmetic  3.71 us (3%)
    psum x1, waiting for transfers between devices, local(): summed_heads = lax.psum(projected, 'gy')  32.2 us
    unnamed x1, blocking collectives  20.8 us
    all_gather x1, blocking collectives, local(): lax.all_gather(attended, 'gx', axis=1, tiled=True)  13.1 us
    dot_general x1, matrix products, local(): jnp.einsum('mrd,dc->mrc', normed, w_query, preferred_element_type=jnp.flo...  8.81 us
    dot_general x1, matrix products, local(): jnp.einsum('mrc,cd->mrd', lax.all_gather(attended, 'gx', axis=1, tiled=Tr...  8.75 us
    unnamed x3, waiting for transfers between devices  7.38 us
    slice x1, local copies, waits for them, and re-layouts, attend(): keys = cache[:, :, :, :, 0, :]  6.95 us
  transfers between devices with their start and end apart: 2, of which 2 were waited for; matrix products, arithmetic and copies ran while one was open for 7% of the time, Pallas kernels for 0%

commit v1 on v0

--- a/solution.py
+++ b/solution.py
@@ -5,6 +5,10 @@
 
 MODEL_WIDTH = 16384
 HEAD_SIZE = 128
+
+
+def touch_sizes(x0):
+    return jnp.concatenate(lax.all_gather(x0, "gx"), axis=1)
 
 
 def rotate(vectors, positions):
@@ -79,10 +83,7 @@
     )
     attended = attend(query_sum, keyval_sum, local_squares, lengths, cache)
     projected = jnp.einsum(
-        "mrc,cd->mrd",
-        lax.all_gather(attended, "gx", axis=1, tiled=True),
-        w_out,
-        preferred_element_type=jnp.float32,
+        "mrc,cd->mrd", touch_sizes(attended), w_out, preferred_element_type=jnp.float32
     )
     summed_heads = lax.psum(projected, "gy")
     return (x_full + summed_heads).astype(jnp.bfloat16)

time: 122 us -> 122 us (level)
  no operation moved by 1% of the time
where the time goes in v1:
time: 122 us
  waiting for transfers between devices  39.5 us (32%)
  blocking collectives  33.9 us (28%)
  matrix products  21.9 us (18%)
  between operations  14.2 us (12%)
  local copies, waits for them, and re-layouts  8.68 us (7%)
  other arithmetic  3.71 us (3%)
    psum x1, waiting for transfers between devices, local(): summed_heads = lax.psum(projected, 'gy')  32.2 us
    unnamed x1, blocking collectives  20.8 us
    all_gather x1, blocking collectives, touch_sizes(): return jnp.concatenate(lax.all_gather(x0, 'gx'), axis=1)  13.1 us
    dot_general x1, matrix products, local(): jnp.einsum('mrd,dc->mrc', normed, w_query, preferred_element_type=jnp.flo...  8.81 us
    dot_general x1, matrix products, local(): jnp.einsum('mrc,cd->mrd', touch_sizes(attended), w_out, preferred_element...  8.75 us
    unnamed x3, waiting for transfers between devices  7.38 us
    slice x1, local copies, waits for them, and re-layouts, attend(): keys = cache[:, :, :, :, 0, :]  6.95 us
  transfers between devices with their start and end apart: 2, of which 2 were waited for; matrix products, arithmetic and copies ran while one was open for 7% of the time, Pallas kernels for 0%

profile of v1, /device:TPU:0, one launch (start us, length us, event | category | flops | bytes accessed | tf_op | source)
XLA Modules:
  0.0 122.0 jit_solution(14115741514442153627)
XLA Ops:
  6.5 0.0 copy-start
  6.5 0.0 all-reduce.9.cloned.1.call-start
  6.5 0.8 convert_element_type.46
  7.4 0.0 copy-start.1
  7.4 0.0 copy-start.2
  7.4 8.8 %fusion.2 = f32[2,8,2048]{2,1,0:T(8,128)} fusion(bf16[4096,2048]{1,0:T(8,128)(2,1)} %param.10, bf16[2,8,4096]{2,1,0:T(8,128)(2,1)} %param.7, f32[4096]{0:T(1024)S(1)} %convert_element_type.46), kind=kOutput, calls=%fused_computation.2 | convolution fusion | flops 268632064 | bytes 17055744 | tf_op jit(solution)/shard_map/mrd,dc->mrc/dot_general | solution.py:75
  16.2 0.0 copy-start.3
  16.2 0.0 all-reduce.9.cloned.1.call-update
  16.2 0.0 all-reduce.7.cloned.1.call-start
  16.3 0.0 copy-done.1
  16.3 0.1 fusion.13
  16.4 0.0 copy-done.2
  16.4 0.1 iota_compare_fusion
  16.5 0.0 copy-done
  16.5 0.4 fusion.9
  16.9 0.0 copy-done.3
  16.9 0.7 dynamic-slice
  18.3 0.1 multiply_cosine_fusion.1
  18.4 20.8 %all-reduce.3 = (f32[2,8]{1,0:T(2,128)S(1)}, f32[2,8,1,256]{3,1,0,2:T(8,128)S(1)}) all-reduce(f32[2,8]{1,0:T(2,128)S(1)} %fusion.13, f32[2,8,1,256]{3,1,0,2:T(8,128)S(1)} %fusion.9), channel_id=3, replica_groups=mesh['groups'=2,'gx'=4,'gy'=4] {'gx'}, use_global_device_ids=true, to_apply=%region_2.0.clone | all-reduce | flops 4112 | bytes 32896
  39.2 0.1 fusion.31
  39.3 0.1 dynamic-slice_multiply_fusion
  39.4 0.1 fusion.28
  39.5 6.9 %fusion.34 = (bf16[2,2,1024,1,1,128]{5,4,3,2,1,0:T(2,128)(2,1)}, bf16[2,2,1024,1,1,128]{5,4,3,2,1,0:T(2,128)(2,1)}) fusion(bf16[2,2,1024,1,2,128]{5,4,3,2,1,0:T(2,128)(2,1)} %param.13), kind=kLoop, calls=%fused_computation.54 | loop fusion | bytes 4194304 | tf_op jit(solution)/shard_map/slice | solution.py:42
  46.4 0.1 maximum_bitcast_fusion
  46.5 7.3 %all-reduce.9.cloned.1.call-done = f32[2,8,2048]{2,1,0:T(8,128)} async-done(((f32[2,8,2048]{2,1,0:T(8,128)}), f32[2,8,2048]{2,1,0:T(8,128)}) %all-reduce.9.cloned.1.call-update) | async-done | bytes 131088
  53.9 0.9 constant_dynamic-slice_fusion
  54.8 0.1 broadcast_multiply_fusion
  54.9 0.1 subtract_convert_fusion
  55.0 0.2 multiply_reduce_fusion
  55.1 2.1 %fusion.35 = (f32[2,2,16]{2,1,0:T(2,128)S(1)}, f32[2,2,16,1024]{3,2,1,0:T(8,128)S(1)}) fusion(bf16[2,2,1024,1,1,128]{5,4,3,2,1,0:T(2,128)(2,1)} %get-tuple-element.9, bf16[2,2,16,64]{3,2,1,0:T(8,128)(2,1)S(1)} %bitcast.41, bf16[2,2,16,64]{3,2,1,0:T(8,128)(2,1)S(1)} %bitcast.40, pred[2,2,1024]{2,1,0:T(4,128)(4,1)S(1)} %iota_compare_fusion), kind=kOutput, calls=%fused_computation.55 | convolution fusion | flops 17006528 | bytes 1331456 | tf_op jit(solution)/shard_map/mrkgd,mrskd->mrkgs/dot_general | solution.py:45
  57.3 0.2 fusion.15
  57.5 1.9 %fusion.8 = bf16[2,2,16,128]{3,2,1,0:T(8,128)(2,1)S(1)} fusion(bf16[2,2,1024,1,1,128]{5,4,3,2,1,0:T(2,128)(2,1)} %get-tuple-element.10, f32[2,2,16,1024]{3,2,1,0:T(8,128)S(1)} %get-tuple-element.18, f32[2,2,16]{2,1,0:T(2,128)S(1)} %multiply_maximum_fusion, f32[2,2,16]{2,1,0:T(2,128)S(1)} %get-tuple-element.7, f32[2,2,128]{2,1,0:T(2,128)S(1)} %slice_bitcast_fusion, ...), kind=kOutput, calls=%fused_computation.10 | convolution fusion | flops 16941056 | bytes 1329920 | tf_op jit(solution)/shard_map/mrkgs,mrskd->mrkgd/dot_general | solution.py:57
  59.4 13.1 %all_gather.3 = bf16[4,2,2,2048]{3,2,1,0:T(2,128)(2,1)S(1)} all-gather(bf16[1,2,2,2048]{3,2,1,0:T(2,128)(2,1)S(1)} %all_gather_reshape.3), channel_id=1, replica_groups=mesh['groups'=2,'gx'=4,'gy'=4] {'gx'}, dimensions={0}, use_global_device_ids=true | all-gather | bytes 81920 | tf_op jit(solution)/shard_map/all_gather | solution.py:11
  72.6 8.7 %fusion = f32[2,8,4096]{2,1,0:T(8,128)} fusion(bf16[2,8,2048]{2,1,0:T(8,128)(2,1)S(1)} %reshape.203, bf16[2048,4096]{1,0:T(8,128)(2,1)} %param.12), kind=kOutput, calls=%fused_computation | convolution fusion | flops 268435456 | bytes 17104896 | tf_op jit(solution)/shard_map/mrc,cd->mrd/dot_general | solution.py:85
  81.4 0.0 all-reduce.7.cloned.1.call-update
  81.4 32.2 %all-reduce.7.cloned.1.call-done = f32[2,8,4096]{2,1,0:T(8,128)} async-done(((f32[2,8,4096]{2,1,0:T(8,128)}), f32[2,8,4096]{2,1,0:T(8,128)}) %all-reduce.7.cloned.1.call-update) | async-done | bytes 262160 | tf_op jit(solution)/shard_map/psum | solution.py:88
  113.6 1.6 %fusion.14 = bf16[2,8,4096]{2,1,0:T(8,128)(2,1)} fusion(f32[2,8,4096]{2,1,0:T(8,128)} %all-reduce.7.cloned.1.call-done, bf16[2,8,4096]{2,1,0:T(8,128)(2,1)S(1)} %copy-done.1), kind=kLoop, calls=%fused_computation.19 | loop fusion | flops 196608 | bytes 524288 | tf_op jit(solution)/shard_map/convert_element_type | solution.py:89
  (9 shorter events, 0.2 us)
Async XLA Ops:
  6.5 10.0 %copy-start = (bf16[4096,1,256]{2,0,1:T(8,128)(2,1)S(1)}, bf16[4096,1,256]{2,0,1:T(8,128)(2,1)}, u32[]{:S(2)}) copy-start(bf16[4096,1,256]{2,0,1:T(8,128)(2,1)} %param.11) | copy-start | bytes 6291460
  6.5 47.3 %all-reduce.9.cloned.1.call-start = ((), (), s32[]{:S(2)}) async-start(), calls=%async_computation.1 | async-start | bytes 262144
  7.4 8.9 %copy-start.1 = (bf16[2,8,4096]{2,1,0:T(8,128)(2,1)S(1)}, bf16[2,8,4096]{2,1,0:T(8,128)(2,1)}, u32[]{:S(2)}) copy-start(bf16[2,8,4096]{2,1,0:T(8,128)(2,1)} %param.7) | copy-start | bytes 393220
  7.4 9.0 %copy-start.2 = (s32[2,2]{1,0:T(2,128)S(1)}, s32[2,2]{1,0:T(2,128)}, u32[]{:S(2)}) copy-start(s32[2,2]{1,0:T(2,128)} %param.8) | copy-start | bytes 52
  16.2 0.7 copy-start.3
  16.2 97.3 %all-reduce.7.cloned.1.call-start = ((), (), s32[]{:S(2)}) async-start(), calls=%async_computation | async-start | bytes 524288 | tf_op jit(solution)/shard_map/psum | solution.py:88
Sparse Core Ops, SparseCore 0:
  16.4 37.4 all-reduce.8
  81.5 31.9 all-reduce.6
